TPU v7x, 32 devices: a 4x4x1 block of a 4x4x8 slice. The times are simulated.
32 devices in a mesh: dp: 1 (over z), tp: 4 (over y), ep: 8 (over x, core).
Axes of the slice: x: 4, y: 4, z: 1, core: 2. Of those that a mesh axis runs over, the one named last changes fastest.
The devices are a block of a 4x4x8 slice.
Arguments:
- tokens: bfloat16 [16384, 2048], P(('dp', 'ep'))
- expert_ids: int32 [16384, 2], P(('dp', 'ep'))
- norm_gain: bfloat16 [2048], replicated
- router_w: bfloat16 [2048, 8], replicated
- w_gate: bfloat16 [8, 2048, 5632], P('ep', None, 'tp')
- w_up: bfloat16 [8, 2048, 5632], P('ep', None, 'tp')
- w_down: bfloat16 [8, 5632, 2048], P('ep', 'tp')
Outputs:
- output: bfloat16 [16384, 2048], P(('dp', 'ep'))
All inputs are finite; a program needn't handle non-finite values.
Results may differ from a plain program's by a relative error of at most 0.014385.
Values are sent between devices in bfloat16 or wider.
A program may use at most 768 MiB of HBM per device.

v0:
```python
import jax
import jax.numpy as jnp
from jax import lax
from jax.sharding import PartitionSpec as P

NORM_EPS = 1e-5


def route_local(tokens, expert_ids, norm_gain, router_w):
    num_tok, top_k = expert_ids.shape
    num_exp = router_w.shape[1]
    slot_cap = 2 * top_k * num_tok // num_exp
    tok_f32 = tokens.astype(jnp.float32)
    inv_rms = lax.rsqrt(jnp.mean(tok_f32 * tok_f32, axis=-1, keepdims=True) + NORM_EPS)
    normed = (tok_f32 * inv_rms * norm_gain.astype(jnp.float32)).astype(jnp.bfloat16)
    logits = jnp.dot(normed, router_w, preferred_element_type=jnp.float32)
    gates = jax.nn.softmax(jnp.take_along_axis(logits, expert_ids, axis=1), axis=-1)
    flat_ids = expert_ids.reshape(-1)
    onehot = (flat_ids[:, None] == jnp.arange(num_exp, dtype=jnp.int32)[None, :]).astype(jnp.int32)
    slot_ids = jnp.sum(jnp.cumsum(onehot, axis=0) * onehot, axis=1) - 1
    dest_pos = flat_ids * slot_cap + slot_ids
    row_tok = jnp.arange(num_tok * top_k, dtype=jnp.int32) // top_k
    src_rows = jnp.zeros((num_exp * slot_cap,), jnp.int32).at[dest_pos].set(row_tok)
    return normed, gates, src_rows, dest_pos


def expert_ffn(rows, w_gate, w_up, w_down):
    gate_act = jnp.einsum('ecd,edf->ecf', rows, w_gate, preferred_element_type=jnp.float32)
    up_act = jnp.einsum('ecd,edf->ecf', rows, w_up, preferred_element_type=jnp.float32)
    hidden = (jax.nn.silu(gate_act) * up_act).astype(jnp.bfloat16)
    return jnp.einsum('ecf,efd->ecd', hidden, w_down, preferred_element_type=jnp.float32).astype(jnp.bfloat16)


def solution(mesh):
    ep_size = mesh.shape['ep']
    tok_spec = P(('dp', 'ep'), None)

    def local_block(tokens, expert_ids, norm_gain, router_w, w_gate, w_up, w_down):
        num_tok, model_dim = tokens.shape
        top_k = expert_ids.shape[1]
        num_exp = router_w.shape[1]
        local_exp = num_exp // ep_size
        slot_cap = 2 * top_k * num_tok // num_exp
        normed, gates, src_rows, dest_pos = route_local(tokens, expert_ids, norm_gain, router_w)
        send_buf = normed[src_rows].reshape(ep_size, local_exp, slot_cap, model_dim)
        recv_buf = lax.all_to_all(send_buf, 'ep', 0, 2, tiled=True)
        recv_buf = recv_buf.reshape(local_exp, ep_size * slot_cap, model_dim)
        part_out = expert_ffn(recv_buf, w_gate, w_up, w_down)
        full_out = lax.psum(part_out, 'tp')
        full_out = full_out.reshape(1, local_exp, ep_size * slot_cap, model_dim)
        back_buf = lax.all_to_all(full_out, 'ep', 2, 0, tiled=True)
        back_buf = back_buf.reshape(num_exp * slot_cap, model_dim)
        picked = back_buf[dest_pos].reshape(num_tok, top_k, model_dim).astype(jnp.float32)
        mixed = jnp.sum(gates[:, :, None] * picked, axis=1)
        return (tokens.astype(jnp.float32) + mixed).astype(jnp.bfloat16)

    return jax.shard_map(local_block, mesh=mesh, in_specs=(tok_spec, tok_spec, P(None), P(None, None), P('ep', None, 'tp'), P('ep', None, 'tp'), P('ep', 'tp', None)), out_specs=tok_spec, check_vma=False)
```

profile of v0, /device:TPU:97, one launch (start us, length us, event | category | flops | bytes accessed | tf_op | source)
XLA Modules:
  0.0 2206.4 jit_solution(15754922276213130004)
XLA Ops:
  6.6 0.7 broadcast_multiply_fusion
  7.3 1.1 copy.41
  8.4 0.5 eq.29
  8.8 0.5 eq.25
  9.3 0.7 convert_element_type.35
  10.0 5.1 fusion
  15.1 0.4 copy.40
  15.5 0.6 mul.63
  16.1 2.3 reduce-window.6
  18.4 0.3 slice_reduce_fusion
  18.8 0.2 reduce-window.9
  18.9 0.1 add_bitcast_fusion
  19.0 0.1 fusion.10
  19.2 0.6 copy-done.4
  19.8 15.5 scatter_custom_fusion
  35.4 8.7 fusion.2
  44.1 65.8 %gather_fusion = bf16[8192,2048]{1,0:T(8,128)(2,1)} fusion(bf16[2048,2048]{1,0:T(8,128)(2,1)} %fusion.2, s32[8192]{0:T(1024)S(1)} %fusion.12), kind=kCustom, calls=%fused_computation | custom fusion | bytes 67141632 | tf_op jit(solution)/shard_map/gather | solution.py:45
  109.9 377.1 %all_to_all.8 = bf16[8,1,1024,2048]{3,2,1,0:T(8,128)(2,1)} all-to-all(bf16[8,1,1024,2048]{3,2,1,0:T(8,128)(2,1)} %bitcast.59), channel_id=1, replica_groups=mesh['dp'=1,'tp'=4,'ep'=8] {'ep'}, dimensions={0} | all-to-all | bytes 67108864 | tf_op jit(solution)/shard_map/all_to_all | solution.py:46
  487.0 60.9 %fusion.7 = f32[8192,1408]{1,0:T(8,128)} fusion(bf16[8192,2048]{1,0:T(8,128)(2,1)} %bitcast.60, bf16[1,2048,1408]{2,1,0:T(8,128)(2,1)} %param.11), kind=kOutput, calls=%fused_computation.17 | convolution fusion | flops 47244640256 | bytes 85458944 | tf_op jit(solution)/shard_map/ecd,edf->ecf/dot_general | solution.py:28
  547.9 0.0 slice-done.1
  548.0 64.3 %multiply_convert_fusion.clone.4 = bf16[8192,1408]{1,0:T(8,128)(2,1)} fusion(f32[8192,1408]{1,0:T(8,128)} %fusion.7, bf16[8192,2048]{1,0:T(8,128)(2,1)} %bitcast.61, bf16[1,2048,1408]{2,1,0:T(8,128)(2,1)S(1)} %bitcast.67), kind=kOutput, calls=%fused_computation.4.clone.clone.clone.1 | convolution fusion | flops 47313846272 | bytes 108527616 | tf_op jit(solution)/shard_map/ecd,edf->ecf/dot_general | solution.py:29
  612.3 59.0 %convert_bitcast_fusion = bf16[1,1,8192,2048]{3,2,1,0:T(8,128)(2,1)} fusion(bf16[1,1408,2048]{2,1,0:T(8,128)(2,1)} %param.13, bf16[8192,1408]{1,0:T(8,128)(2,1)} %multiply_convert_fusion.clone.4), kind=kOutput, calls=%fused_computation.7 | convolution fusion | flops 47261417472 | bytes 62390272 | tf_op jit(solution)/shard_map/ecf,efd->ecd/dot_general | solution.py:31
  671.3 0.1 all-reduce.2.cloned.1.call-update
  671.3 560.7 %all-reduce.2.cloned.1.call-done = bf16[1,1,8192,2048]{3,2,1,0:T(8,128)(2,1)} async-done(((bf16[1,1,8192,2048]{3,2,1,0:T(8,128)(2,1)}), bf16[1,1,8192,2048]{3,2,1,0:T(8,128)(2,1)}) %all-reduce.2.cloned.1.call-update) | async-done | bytes 33554448 | tf_op jit(solution)/shard_map/psum | solution.py:49
  1232.1 56.6 %copy.51 = bf16[1,1,8192,2048]{3,1,0,2:T(2,128)(2,1)} copy(bf16[1,1,8192,2048]{3,2,1,0:T(8,128)(2,1)} %all-reduce.2.cloned.1.call-done) | data formatting | bytes 67108864 | tf_op jit(solution)/shard_map/psum | solution.py:49
  1288.7 0.6 broadcast.148
  1289.3 196.0 %reduce.2 = bf16[8192,2048]{1,0:T(8,128)(2,1)} reduce(bf16[8192,1,1,2048]{3,2,1,0:T(2,128)(2,1)} %bitcast.55, bf16[]{:T(256)} %broadcast.148), dimensions={1,2}, to_apply=%bitcast.55.reduce_sub_computation | reduce | bytes 67108864
  1485.3 30.7 %reshape.188 = bf16[8,2,1048576]{2,1,0:T(2,128)(2,1)} reshape(bf16[8192,2048]{1,0:T(8,128)(2,1)} %reduce.2) | data formatting | bytes 67108864
  1516.0 8.4 all-to-all-start.1
  1524.4 0.0 copy-done.2
  1524.5 0.4 copy.37
  1524.8 0.5 reshape.165
  1525.3 0.0 copy-done
  1525.3 5.6 fusion.22
  1531.0 24.5 %gather_fusion.2 = f32[4096]{0:T(1024)S(1)} fusion(f32[2048,8]{0,1:T(8,128)S(1)} %fusion.22, s32[4096]{0:T(1024)S(1)} %reshape.165), kind=kCustom, calls=%fused_computation.2 | custom fusion | bytes 65536 | tf_op jit(solution)/shard_map/jit(take_along_axis)/gather | solution.py:17
  1555.5 1.0 reshape.168
  1556.5 0.3 copy.38
  1556.8 0.0 copy-done.3
  1557.0 0.4 copy.39
  1557.4 330.2 %all-to-all-done.1 = bf16[8,2,1048576]{2,1,0:T(2,128)(2,1)} async-done(((bf16[8,2,1048576]{2,1,0:T(2,128)(2,1)}), bf16[8,2,1048576]{2,1,0:T(2,128)(2,1)}, u32[]{:S(2)}, u32[]{:S(2)}) %all-to-all-start.1) | async-done | bytes 33554464 | tf_op jit(solution)/shard_map/all_to_all | solution.py:51
  1887.5 71.2 %reshape.189 = bf16[8192,1,1,2048]{3,2,1,0:T(2,128)(2,1)} reshape(bf16[8,2,1048576]{2,1,0:T(2,128)(2,1)} %all-to-all-done.1) | data formatting | bytes 67108864
  1958.7 41.1 %copy.50 = bf16[1,1,8192,2048]{3,2,0,1:T(8,128)(2,1)} copy(bf16[1,1,8192,2048]{3,1,0,2:T(2,128)(2,1)} %bitcast.39) | data formatting | bytes 67108864
  1999.8 95.6 %gather_fusion.1 = bf16[4096,2048]{1,0:T(8,128)(2,1)} fusion(bf16[8192,2048]{1,0:T(8,128)(2,1)} %bitcast.58, s32[4096]{0:T(1024)S(1)} %broadcast_clamp_fusion), kind=kCustom, calls=%fused_computation.1 | custom fusion | bytes 33570816 | tf_op jit(solution)/shard_map/gather | solution.py:53
  2095.4 35.3 %reshape.148 = f32[2048,2,2048]{2,1,0:T(2,128)} reshape(bf16[4096,2048]{1,0:T(8,128)(2,1)} %gather_fusion.1) | data formatting | bytes 50331648 | tf_op jit(solution)/shard_map/convert_element_type | solution.py:53
  2130.7 0.0 copy-start.1
  2130.8 56.3 %multiply_reduce_fusion = f32[2048,2048]{1,0:T(8,128)} fusion(f32[2048,2,2048]{2,1,0:T(2,128)} %reshape.148, f32[2048,2]{1,0:T(8,128)S(1)} %copy.39), kind=kLoop, calls=%fused_computation.6 | loop fusion | flops 12582912 | bytes 50348032 | tf_op jit(solution)/shard_map/reduce_sum | solution.py:54
  2187.1 12.0 fusion.3
  2199.0 0.0 copy-done.1
  (22 shorter events, 0.2 us)
Async XLA Ops:
  6.5 1518.8 %copy-start = (bf16[2048,8]{0,1:T(8,128)(2,1)S(1)}, bf16[2048,8]{0,1:T(8,128)(2,1)}, u32[]{:S(2)}) copy-start(bf16[2048,8]{0,1:T(8,128)(2,1)} %param.10) | copy-start | bytes 98308
  6.6 1225.5 %all-reduce.2.cloned.1.call-start = ((), (), s32[]{:S(2)}) async-start(), calls=%async_computation.2 | async-start | bytes 67108864 | tf_op jit(solution)/shard_map/psum | solution.py:49
  19.2 0.6 copy-start.4
  109.9 438.0 %slice-start = ((s8[5767168]{0:T(1024)(128)(4,1)}), s8[4194304]{0:T(1024)(128)(4,1)S(1)}, s32[]{:S(2)}) async-start(s8[5767168]{0:T(1024)(128)(4,1)} %bitcast.66), calls=%async_computation.3 | async-start | bytes 8388608
  487.0 60.9 %slice-start.1 = ((s8[5767168]{0:T(1024)(128)(4,1)}), s8[1572864]{0:T(1024)(128)(4,1)S(1)}, s32[]{:S(2)}) async-start(s8[5767168]{0:T(1024)(128)(4,1)} %bitcast.66), calls=%async_computation.4 | async-start | bytes 3145728
  1516.0 8.5 copy-start.2
  1516.0 371.6 %all-to-all-start.1 = ((bf16[8,2,1048576]{2,1,0:T(2,128)(2,1)}), bf16[8,2,1048576]{2,1,0:T(2,128)(2,1)}, u32[]{:S(2)}, u32[]{:S(2)}) async-start(bf16[8,2,1048576]{2,1,0:T(2,128)(2,1)} %reshape.188), calls=%async_computation.1 | async-start | bytes 67108864 | tf_op jit(solution)/shard_map/all_to_all | solution.py:51
  1531.0 25.9 %copy-start.3 = (s32[2048,2]{0,1:T(2,128)S(1)}, s32[2048,2]{0,1:T(2,128)}, u32[]{:S(2)}) copy-start(s32[2048,2]{0,1:T(2,128)} %param.8) | copy-start | bytes 49156
  1531.0 26.4 %copy-start.5 = (s32[4096,1]{0,1:T(1,128)S(1)}, s32[4096,1]{0,1:T(1,128)}, u32[]{:S(2)}) copy-start(s32[4096,1]{0,1:T(1,128)} %copy-done.4) | copy-start | bytes 49156
  2130.7 68.3 %copy-start.1 = (bf16[2048,8]{0,1:T(8,128)(2,1)S(1)}, bf16[2048,8]{0,1:T(8,128)(2,1)}, u32[]{:S(2)}) copy-start(bf16[2048,8]{0,1:T(8,128)(2,1)} %param.10) | copy-start | bytes 98308
Sparse Core Ops, SparseCore 0:
  671.5 560.5 all-reduce.1
where the time goes:
time: 2220 us; the launch traced here: 2210 us
  waiting for transfers between devices  891 us (40%)
  local copies, waits for them, and re-layouts  443 us (20%)
  blocking collectives  377 us (17%)
  other arithmetic  282 us (13%)
  matrix products  190 us (9%)
    psum x1, waiting for transfers between devices, local_block(): full_out = lax.psum(part_out, 'tp')  561 us
    all_to_all x1, blocking collectives, local_block(): recv_buf = lax.all_to_all(send_buf, 'ep', 0, 2, tiled=True)  377 us
    all_to_all x1, waiting for transfers between devices, local_block(): back_buf = lax.all_to_all(full_out, 'ep', 2, 0, tiled=True)  330 us
    unnamed x3, other arithmetic  196 us
    unnamed x21, local copies, waits for them, and re-layouts  145 us
    gather x1, local copies, waits for them, and re-layouts, local_block(): back_buf[dest_pos].reshape(num_tok, top_k, model_dim).astype(jnp.float32)  95.6 us
    gather x1, local copies, waits for them, and re-layouts, local_block(): send_buf = normed[src_rows].reshape(ep_size, local_exp, slot_cap, model_dim)  65.8 us
    dot_general x1, matrix products, expert_ffn(): jnp.einsum('ecd,edf->ecf', rows, w_up, preferred_element_type=jnp.float32)  64.3 us
  transfers between devices with their start and end apart: 2, of which 2 were waited for; matrix products, arithmetic and copies ran while one was open for 1% of the time, Pallas kernels for 0%

commit v1 on v0

v1 whole, which is shorter than its diff:
```python
import functools

import jax
import jax.numpy as jnp
from jax import lax
from jax.experimental import pallas as pl
from jax.experimental.pallas import tpu as pltpu
from jax.sharding import PartitionSpec as P


NORM_EPS = 1e-5
GROUPS = (((512, 512), True), ((512,), False), ((512,), False))
PIECES = sum((sizes for sizes, _ in GROUPS), ())
CHUNK = 256
ALIGN = 16
WIN = CHUNK + ALIGN
SHARE = 128
ORDER = ("A1", "A2", "F0", "F1", "F2", "S0", "F3", "S1", "S2", "S3", "M0123")
LEVELS = ((1536, 304, (128, True), (192, 2)), (1792, 320, (128, 1), (128, 1)))
SPARE_TILE = 128
LANES = 128


def rms_norm(x_ref, gain_ref):
    x = x_ref[...].astype(jnp.float32)
    inv = lax.rsqrt(jnp.mean(x * x, axis=-1, keepdims=True) + NORM_EPS)
    return (x * inv * gain_ref[...].astype(jnp.float32)).astype(jnp.bfloat16)


def norm_kernel(at_ref, x_ref, gain_ref, h_ref):
    h_ref[...] = rms_norm(x_ref, gain_ref)


def norm_rows(begin, rows, share, tokens, gain, blk=64):
    dim = tokens.shape[1]
    return pl.pallas_call(
        norm_kernel,
        grid_spec=pltpu.PrefetchScalarGridSpec(
            num_scalar_prefetch=1,
            grid=(rows // blk,),
            in_specs=[
                pl.BlockSpec((blk, dim), lambda i, at: (begin // blk + at[0] * (rows // blk) + i, 0)),
                pl.BlockSpec((1, dim), lambda i, at: (0, 0)),
            ],
            out_specs=pl.BlockSpec((blk, dim), lambda i, at: (i, 0)),
        ),
        out_shape=pltpu.HBM((rows, dim), jnp.bfloat16),
        cost_estimate=pl.CostEstimate(flops=8 * rows * dim, bytes_accessed=4 * rows * dim, transcendentals=0),
        name="norm",
    )(share, tokens, gain)


def gate_kernel(x_ref, ids_ref, gain_ref, rw_ref, gate_ref):
    logits = jnp.dot(rms_norm(x_ref, gain_ref), rw_ref[...], preferred_element_type=jnp.float32)
    lane = lax.broadcasted_iota(jnp.int32, logits.shape, 1)
    ids = ids_ref[...]
    l0 = jnp.sum(jnp.where(lane == ids[:, 0:1], logits, 0.0), axis=-1, keepdims=True)
    l1 = jnp.sum(jnp.where(lane == ids[:, 1:2], logits, 0.0), axis=-1, keepdims=True)
    top = jnp.maximum(l0, l1)
    e0, e1 = jnp.exp(l0 - top), jnp.exp(l1 - top)
    tot = e0 + e1
    gate_ref[...] = jnp.where(lane == 0, e0 / tot, jnp.where(lane == 1, e1 / tot, 0.0))


def gate_rows(tokens, ids, gain, rw):
    rows, dim = tokens.shape
    blk = 64
    return pl.pallas_call(
        gate_kernel,
        grid=(rows // blk,),
        in_specs=[
            pl.BlockSpec((blk, dim), lambda i: (i, 0)),
            pl.BlockSpec((blk, ids.shape[1]), lambda i: (i, 0)),
            pl.BlockSpec((1, dim), lambda i: (0, 0)),
            pl.BlockSpec((dim, LANES), lambda i: (0, 0)),
        ],
        out_specs=pl.BlockSpec((blk, LANES), lambda i: (i, 0)),
        out_shape=jax.ShapeDtypeStruct((rows, LANES), jnp.float32),
        cost_estimate=pl.CostEstimate(flops=2 * rows * dim * LANES, bytes_accessed=2 * rows * dim, transcendentals=0),
        name="gate",
    )(tokens, ids, gain, rw)


def ffn_kernel(unroll, tile_rows, rows_of, per_block, meta_ref, pos_ref, hall_ref, w13_hbm, w2_hbm, y_ref,
               w13_ref, w2_ref, rows_s, u_s, hbuf, obuf, wsem, hsem, osem):
    chunks = pos_ref.shape[0]
    nup, _, pair = w13_ref.shape
    half = pair // 2
    ndown, _, wide = w2_ref.shape
    slots = hbuf.shape[0]

    def fetch(j):
        slot = lax.rem(j, slots)
        row = pl.multiple_of((j // per_block) * rows_of[0] + rows_of[1] + lax.rem(j, per_block) * CHUNK, CHUNK)
        return pltpu.make_async_copy(hall_ref.at[pl.ds(row, CHUNK)], hbuf.at[slot], hsem.at[slot])

    for j in range(slots - 1):
        fetch(j).start()
    weights = [pltpu.make_async_copy(w13_hbm, w13_ref, wsem.at[0]), pltpu.make_async_copy(w2_hbm, w2_ref, wsem.at[1])]
    for w in weights:
        w.start()

    def compact(j, carry):
        @pl.when(j + slots - 1 < chunks)
        def _():
            fetch(j + slots - 1).start()

        fetch(j).wait()
        slot = lax.rem(j, slots)
        start = pl.multiple_of(meta_ref[j], ALIGN)
        rel = pos_ref[j] - start
        pick = (lax.broadcasted_iota(jnp.int32, (WIN, CHUNK), 0) == rel).astype(jnp.bfloat16)
        got = jnp.dot(pick, hbuf[slot], preferred_element_type=jnp.float32).astype(jnp.bfloat16)
        old = rows_s[pl.ds(start, ALIGN), :]
        old = jnp.where(lax.rem(j, per_block) == 0, jnp.zeros_like(old), old)
        rows_s[pl.ds(start, ALIGN), :] = old + got[:ALIGN]
        rows_s[pl.ds(start + ALIGN, CHUNK), :] = got[ALIGN:]
        return carry

    lax.fori_loop(0, chunks, compact, 0)
    for w in weights:
        w.wait()

    def put(i):
        slot = lax.rem(i, 2)
        return pltpu.make_async_copy(obuf.at[slot], y_ref.at[pl.ds(pl.multiple_of(i * tile_rows, ALIGN), tile_rows)], osem.at[slot])

    tiles = meta_ref[chunks]

    def tile(i, carry):
        slot = lax.rem(i, 2)
        a = rows_s[pl.ds(pl.multiple_of(i * tile_rows, ALIGN), tile_rows), :]

        def up_step(j, c):
            both = jnp.dot(a, w13_ref[j], preferred_element_type=jnp.float32)
            act, up = both[:, :half], both[:, half:]
            u_s[:, pl.ds(pl.multiple_of(j * half, half), half)] = (jax.nn.silu(act) * up).astype(jnp.bfloat16)
            return c

        lax.fori_loop(0, nup, up_step, 0, unroll=unroll)

        @pl.when(i >= 2)
        def _():
            put(i - 2).wait()

        u = u_s[...]

        def down_step(j, c):
            obuf[slot, :, pl.ds(pl.multiple_of(j * wide, wide), wide)] = jnp.dot(
                u, w2_ref[j], preferred_element_type=jnp.float32
            ).astype(jnp.bfloat16)
            return c

        lax.fori_loop(0, ndown, down_step, 0, unroll=unroll)
        put(i).start()
        return carry

    lax.fori_loop(0, tiles, tile, 0)

    @pl.when(tiles >= 2)
    def _():
        put(tiles - 2).wait()

    @pl.when(tiles >= 1)
    def _():
        put(tiles - 1).wait()


def ffn_piece(unroll, cap, tile_rows, rows_of, per_block, meta, pos, hall, w13, w2):
    dim, width = w13.shape[1], w2.shape[1]
    slots = 4
    hbm = pl.BlockSpec(memory_space=pltpu.HBM)
    vmem = pl.BlockSpec(memory_space=pltpu.VMEM)
    scratch = 2 * dim * (cap + WIN + slots * CHUNK + 2 * tile_rows) + 2 * tile_rows * width
    return pl.pallas_call(
        functools.partial(ffn_kernel, unroll, tile_rows, rows_of, per_block),
        in_specs=[pl.BlockSpec(memory_space=pltpu.SMEM), vmem, hbm, hbm, hbm],
        out_specs=hbm,
        scratch_shapes=[
            pltpu.VMEM(w13.shape, w13.dtype),
            pltpu.VMEM(w2.shape, w2.dtype),
            pltpu.VMEM((cap + WIN, dim), jnp.bfloat16),
            pltpu.VMEM((tile_rows, width), jnp.bfloat16),
            pltpu.VMEM((slots, CHUNK, dim), jnp.bfloat16),
            pltpu.VMEM((2, tile_rows, dim), jnp.bfloat16),
            pltpu.SemaphoreType.DMA((2,)),
            pltpu.SemaphoreType.DMA((slots,)),
            pltpu.SemaphoreType.DMA((2,)),
        ],
        out_shape=pltpu.HBM((cap, dim), jnp.bfloat16),
        compiler_params=pltpu.CompilerParams(vmem_limit_bytes=scratch + 2 * (w13.size + w2.size) + 6 * 1024 * 1024),
        cost_estimate=pl.CostEstimate(
            flops=6 * (cap * 3 // 4) * dim * width, bytes_accessed=2 * (hall.size + cap * dim), transcendentals=0
        ),
        name="ffn",
    )(meta, pos, *(pltpu.with_memory_space_constraint(a, pltpu.HBM) for a in (hall, w13, w2)))


def pair_kernel(w1_ref, w3_ref, out_ref):
    half = w1_ref.shape[1]
    out_ref[0, :, :half] = w1_ref[...]
    out_ref[0, :, half:] = w3_ref[...]


def pair_columns(w1, w3):
    dim, width = w1.shape
    return pl.pallas_call(
        pair_kernel,
        grid=(width // LANES,),
        in_specs=[pl.BlockSpec((dim, LANES), lambda j: (0, j))] * 2,
        out_specs=pl.BlockSpec((1, dim, 2 * LANES), lambda j: (j, 0, 0)),
        out_shape=pltpu.HBM((width // LANES, dim, 2 * LANES), w1.dtype),
        cost_estimate=pl.CostEstimate(flops=8 * dim * width, bytes_accessed=8 * dim * width, transcendentals=0),
        name="pair",
    )(w1, w3)


def block_kernel(w_ref, out_ref):
    out_ref[0] = w_ref[...]


def block_columns(w):
    width, dim = w.shape
    wide = 2 * LANES
    return pl.pallas_call(
        block_kernel,
        grid=(dim // wide,),
        in_specs=[pl.BlockSpec((width, wide), lambda j: (0, j))],
        out_specs=pl.BlockSpec((1, width, wide), lambda j: (j, 0, 0)),
        out_shape=pltpu.HBM((dim // wide, width, wide), w.dtype),
        cost_estimate=pl.CostEstimate(flops=4 * dim * width, bytes_accessed=4 * dim * width, transcendentals=0),
        name="block",
    )(w)


def spread_kernel(cap_slots, meta_ref, y_ref, out_ref):
    blocks = out_ref.shape[0] // cap_slots
    cols = out_ref.shape[1]

    def clear(g, carry):
        out_ref[pl.ds(pl.multiple_of(g * ALIGN, ALIGN), ALIGN), :] = jnp.zeros((ALIGN, cols), out_ref.dtype)
        return carry

    lax.fori_loop(0, out_ref.shape[0] // ALIGN, clear, 0, unroll=8)
    for s in range(blocks):
        def body(g, carry):
            src = pl.multiple_of(meta_ref[s] + g * ALIGN, ALIGN)
            dst = pl.multiple_of(s * cap_slots + g * ALIGN, ALIGN)
            out_ref[pl.ds(dst, ALIGN), :] = y_ref[pl.ds(src, ALIGN), :]
            return carry

        lax.fori_loop(0, meta_ref[blocks + s], body, 0)


def spread_piece(cap_slots, blocks, meta, y):
    cap, cols = y.shape
    return pl.pallas_call(
        functools.partial(spread_kernel, cap_slots),
        grid_spec=pltpu.PrefetchScalarGridSpec(
            num_scalar_prefetch=1,
            grid=(1,),
            in_specs=[pl.BlockSpec((cap, cols), lambda i, m: (0, 0))],
            out_specs=pl.BlockSpec((blocks * cap_slots, cols), lambda i, m: (0, 0)),
        ),
        out_shape=pltpu.HBM((blocks * cap_slots, cols), y.dtype),
        cost_estimate=pl.CostEstimate(flops=1 << 20, bytes_accessed=4 * (cap + blocks * cap_slots) * cols, transcendentals=0),
        name="spread",
    )(meta, y)


def mix_kernel(col_ref, rows_ref, x_ref, slot_ref, gate_ref, out_ref, both_s):
    toks = x_ref.shape[0]
    experts, slots, _ = rows_ref.shape
    lane = lax.broadcasted_iota(jnp.int32, (toks, slots), 1)
    q = slot_ref[...]
    both_s[...] = jnp.zeros_like(both_s)

    def expert(e, carry):
        at = lane + e * slots
        pick = jnp.concatenate([(at == q[:, k : k + 1]).astype(jnp.bfloat16) for k in range(2)], axis=0)
        both_s[...] += jnp.dot(pick, rows_ref[e], preferred_element_type=jnp.float32)
        return carry

    lax.fori_loop(0, experts, expert, 0)
    mixed = gate_ref[:, 0:1] * both_s[:toks, :] + gate_ref[:, 1:2] * both_s[toks:, :]
    out_ref[...] = (x_ref[...].astype(jnp.float32) + mixed).astype(out_ref.dtype)


def mix_piece(toks, at, rows, tokens, slot, gate):
    experts, slots, cols = rows.shape
    blk = 64
    return pl.pallas_call(
        mix_kernel,
        grid_spec=pltpu.PrefetchScalarGridSpec(
            num_scalar_prefetch=1,
            grid=(toks // blk,),
            in_specs=[
                pl.BlockSpec((experts, slots, cols), lambda i, at: (0, 0, 0)),
                pl.BlockSpec((blk, cols), lambda i, at: (at[1] * (toks // blk) + i, at[0])),
                pl.BlockSpec((blk, 2), lambda i, at: (i, 0)),
                pl.BlockSpec((blk, LANES), lambda i, at: (at[1] * (toks // blk) + i, 0)),
            ],
            out_specs=pl.BlockSpec((blk, cols), lambda i, at: (i, 0)),
            scratch_shapes=[pltpu.VMEM((2 * blk, cols), jnp.float32)],
        ),
        out_shape=jax.ShapeDtypeStruct((toks, cols), tokens.dtype),
        compiler_params=pltpu.CompilerParams(vmem_limit_bytes=40 * 1024 * 1024),
        cost_estimate=pl.CostEstimate(flops=4 * toks * rows.size, bytes_accessed=2 * (rows.size + 2 * toks * cols), transcendentals=0),
        name="mix",
    )(at, rows, tokens, slot, gate)


def mix_share_kernel(peers, homes, count, *refs):
    rows_refs, away_ref = refs[: count - 1], refs[count - 1]
    slot_ref, gate_ref, x_ref, out_ref, x_s, o_s, rows_s = refs[count : count + 7]
    rows_sem, x_sem, own_sem, send_sem, recv_sem, pass_sem, passed_sem, stay_sem, go_sem, come_sem = refs[count + 7 :]
    toks, cols = o_s.shape
    blk = SHARE
    blocks = toks // blk
    me, here_e = lax.axis_index("tp"), lax.axis_index("ep")
    sides = (lax.rem(me + 1, peers), lax.rem(me + peers - 1, peers))

    def columns(owner):
        return pl.ds(pl.multiple_of(owner * cols, cols), cols)

    fetch = pltpu.make_async_copy(x_ref.at[:, columns(me)], x_s, x_sem)
    fetch.start()
    loads = [pltpu.make_async_copy(ref, rows_s.at[n], rows_sem.at[n]) for n, ref in enumerate(rows_refs)]
    for load in loads:
        load.start()
    barrier = pltpu.get_barrier_semaphore()
    for side in sides:
        pl.semaphore_signal(barrier, inc=1, device_id={"tp": side}, device_id_type=pl.DeviceIdType.MESH)
    for r in range(1, homes):
        other = lax.rem(here_e + r, homes)
        pl.semaphore_signal(barrier, inc=1, device_id={"ep": other}, device_id_type=pl.DeviceIdType.MESH)
    pl.semaphore_wait(barrier, homes + 1)

    slots = away_ref.shape[1]
    mine_e = pl.ds(pl.multiple_of(here_e * slots, ALIGN), slots)
    stay = pltpu.make_async_copy(away_ref.at[here_e], rows_s.at[count - 1, mine_e], stay_sem)
    stay.start()
    trips = []
    for r in range(1, homes):
        other = lax.rem(here_e + r, homes)
        trips.append(
            pltpu.make_async_remote_copy(
                src_ref=away_ref.at[other], dst_ref=rows_s.at[count - 1, mine_e],
                send_sem=go_sem.at[r - 1], recv_sem=come_sem.at[r - 1],
                device_id={"ep": other}, device_id_type=pl.DeviceIdType.MESH,
            )
        )
        trips[-1].start()
    fetch.wait()
    for load in loads:
        load.wait()

    def own(b):
        here = pl.ds(pl.multiple_of(b * blk, blk), blk)
        return pltpu.make_async_copy(o_s.at[here], out_ref.at[here, columns(me)], own_sem.at[b])

    def send(k, b):
        here = pl.ds(pl.multiple_of(b * blk, blk), blk)
        return pltpu.make_async_remote_copy(
            src_ref=o_s.at[here], dst_ref=out_ref.at[here, columns(me)],
            send_sem=send_sem.at[k, b], recv_sem=recv_sem.at[k, b],
            device_id={"tp": sides[k]}, device_id_type=pl.DeviceIdType.MESH,
        )

    def hand_on(k, b):
        half = pl.ds(pl.multiple_of(b * blk + k * (blk // 2), blk // 2), blk // 2)
        part = out_ref.at[half, columns(sides[1 - k])]
        return pltpu.make_async_remote_copy(
            src_ref=part, dst_ref=part,
            send_sem=pass_sem.at[k, b], recv_sem=passed_sem.at[k, b],
            device_id={"tp": sides[k]}, device_id_type=pl.DeviceIdType.MESH,
        )

    def relay(b):
        for k in range(2):
            send(k, b).wait_recv()
            hand_on(k, b).start()

    steps = blocks // count
    lane = lax.broadcasted_iota(jnp.int32, (blk, rows_s.shape[1]), 1)

    def block(b, carry):
        here = pl.ds(pl.multiple_of(b * blk, blk), blk)

        @pl.when(b == blocks - steps)
        def _():
            stay.wait()
            for trip in trips:
                trip.wait()

        q = slot_ref[here, :]
        gate = gate_ref[here, :]
        mixed = jnp.zeros((blk, cols), jnp.float32)
        for k in range(2):
            pick = (lane == q[:, k : k + 1]).astype(jnp.bfloat16)
            mixed += gate[:, k : k + 1] * jnp.dot(pick, rows_s[b // steps], preferred_element_type=jnp.float32)
        o_s[here, :] = (x_s[here, :].astype(jnp.float32) + mixed).astype(o_s.dtype)
        own(b).start()
        for k in range(2):
            send(k, b).start()

        @pl.when(b > 0)
        def _():
            relay(b - 1)

        return carry

    lax.fori_loop(0, blocks, block, 0)
    relay(blocks - 1)

    def finish(b, carry):
        own(b).wait()
        for k in range(2):
            send(k, b).wait_send()
            hand_on(k, b).wait()
        return carry

    lax.fori_loop(0, blocks, finish, 0)


def mix_share(peers, rows, away, tokens, slot, gate, name_id):
    assert peers == 4 and len(set(PIECES)) == 1
    homes, _, cols = away.shape
    toks = tokens.shape[0]
    blocks = toks // SHARE
    count = len(rows) + 1
    vmem, hbm = pl.BlockSpec(memory_space=pltpu.VMEM), pl.BlockSpec(memory_space=pl.ANY)
    return pl.pallas_call(
        functools.partial(mix_share_kernel, peers, homes, count),
        in_specs=[hbm] * count + [vmem, vmem, hbm],
        out_specs=hbm,
        out_shape=pltpu.HBM(tokens.shape, tokens.dtype),
        scratch_shapes=[
            pltpu.VMEM((toks, cols), tokens.dtype),
            pltpu.VMEM((toks, cols), tokens.dtype),
            pltpu.VMEM((count, homes * away.shape[1], cols), away.dtype),
            pltpu.SemaphoreType.DMA((count - 1,)),
            pltpu.SemaphoreType.DMA,
            pltpu.SemaphoreType.DMA((blocks,)),
        ]
        + [pltpu.SemaphoreType.DMA((2, blocks))] * 4
        + [pltpu.SemaphoreType.DMA, pltpu.SemaphoreType.DMA((homes - 1,)), pltpu.SemaphoreType.DMA((homes - 1,))],
        compiler_params=pltpu.CompilerParams(
            collective_id=name_id, has_side_effects=True, vmem_limit_bytes=40 * 1024 * 1024
        ),
        cost_estimate=pl.CostEstimate(flops=4 * toks * away.size, bytes_accessed=16 * toks * cols, transcendentals=0),
    )(*rows, pltpu.with_memory_space_constraint(away, pltpu.HBM), slot, gate, tokens)


def tell_kernel(homes, ids_ref, all_ref, own_sem, send_sem, recv_sem):
    me = lax.axis_index("ep")
    others = [lax.rem(me + r, homes) for r in range(1, homes)]
    barrier = pltpu.get_barrier_semaphore()
    for other in others:
        pl.semaphore_signal(barrier, inc=1, device_id={"ep": other}, device_id_type=pl.DeviceIdType.MESH)
    pl.semaphore_wait(barrier, homes - 1)
    copies = [pltpu.make_async_copy(ids_ref, all_ref.at[me], own_sem)]
    for r, other in enumerate(others):
        copies.append(
            pltpu.make_async_remote_copy(
                src_ref=ids_ref, dst_ref=all_ref.at[me], send_sem=send_sem.at[r], recv_sem=recv_sem.at[r],
                device_id={"ep": other}, device_id_type=pl.DeviceIdType.MESH,
            )
        )
    for copy in copies:
        copy.start()
    for copy in copies:
        copy.wait()


def tell_ids(homes, ids, name_id):
    anyspec = pl.BlockSpec(memory_space=pl.ANY)
    dma = pltpu.SemaphoreType.DMA
    return pl.pallas_call(
        functools.partial(tell_kernel, homes),
        in_specs=[anyspec],
        out_specs=anyspec,
        out_shape=pltpu.HBM((homes, *ids.shape), ids.dtype),
        scratch_shapes=[dma, dma((homes - 1,)), dma((homes - 1,))],
        compiler_params=pltpu.CompilerParams(collective_id=name_id, has_side_effects=True),
        cost_estimate=pl.CostEstimate(flops=1 << 20, bytes_accessed=2 * homes * ids.size * 4, transcendentals=0),
        name="tell",
    )(pltpu.with_memory_space_constraint(ids, pltpu.HBM))


def unwritten(like):
    return pl.pallas_call(
        lambda out_ref: None,
        out_specs=pl.BlockSpec(memory_space=pl.ANY),
        out_shape=pltpu.HBM(like.shape, like.dtype),
        name="unwritten",
    )()


def after(x, *earlier):
    return lax.optimization_barrier((x, *earlier))[0]


def solution(mesh):
    tp, ep = mesh.shape["tp"], mesh.shape["ep"]
    tok_spec = P(("dp", "ep"), None)

    def local_block(tokens, ids, gain, router_w, w_gate, w_up, w_down):
        num_tok, dim = tokens.shape
        num_exp = router_w.shape[1]
        assert num_exp == ep and ids.shape[1] == 2
        assert sum(PIECES) == num_tok
        begin = [sum(PIECES[:p]) for p in range(len(PIECES))]
        gain2 = gain.reshape(1, dim)
        rw = jnp.pad(router_w, ((0, 0), (0, LANES - num_exp)))
        me, col = lax.axis_index("ep"), lax.axis_index("tp")
        cols = dim // tp

        home = [(g, sum(sizes[:i])) for g, (sizes, _) in enumerate(GROUPS) for i in range(len(sizes))]
        group_begin = [begin[[h[0] for h in home].index(g)] for g in range(len(GROUPS))]

        def norm_group(g):
            size, wide = sum(GROUPS[g][0]), GROUPS[g][1]
            if wide:
                return norm_rows(group_begin[g], size // tp, col.reshape(1), tokens, gain2, 128)
            return norm_rows(group_begin[g], size, jnp.zeros((1,), jnp.int32), tokens, gain2)

        def gather_group(g, h):
            return lax.all_gather(h, ("ep", "tp") if GROUPS[g][1] else "ep", axis=0, tiled=True)

        normed = [norm_group(g) for g in range(len(GROUPS))]
        hall0 = gather_group(0, normed[0])
        gates = gate_rows(tokens, ids, gain2, rw)

        w13, w2 = pair_columns(w_gate[0], w_up[0]), block_columns(w_down[0])

        ids_t = ids.T
        all_ids = tell_ids(ep, ids_t, len(LEVELS))
        experts = jnp.arange(num_exp, dtype=jnp.int32)
        earlier = jnp.arange(ep)[None, :] < jnp.arange(ep)[:, None]
        most_rows, most_slots = [], []
        positions, fast_meta, full_meta, fast_rows, full_rows = [], [], [], [], []
        for p, (b, n) in enumerate(zip(begin, PIECES)):
            before = (jnp.arange(n)[:, None] < jnp.arange(n)[None, :]).astype(jnp.bfloat16)

            def rank(mask):
                return jnp.dot(mask.astype(jnp.bfloat16), before, preferred_element_type=jnp.float32).astype(jnp.int32)

            piece = all_ids[:, :, b : b + n]
            hit = (piece[None] == experts[:, None, None, None]).any(axis=2)
            load = jnp.sum(hit.astype(jnp.int32), axis=-1)
            padded = (load + ALIGN - 1) // ALIGN * ALIGN
            most_rows.append(jnp.max(jnp.sum(padded, axis=1)))
            most_slots.append(jnp.max(load))

            mine = (piece == me).any(axis=1)
            my_pad = (jnp.sum(mine.astype(jnp.int32), axis=-1) + ALIGN - 1) // ALIGN * ALIGN
            base = jnp.sum(jnp.where(earlier, my_pad[None, :], 0), axis=-1)
            pos = base[:, None] + rank(mine)
            starts = pos[:, ::CHUNK].reshape(-1) // ALIGN * ALIGN
            pos = jnp.where(mine, pos, -1).reshape(ep * n // CHUNK, 1, CHUNK)

            def limits(cap, slots, *tilings):
                tile_rows = tilings[min(p, len(tilings) - 1)][0]
                tiles = jnp.minimum((jnp.sum(my_pad) + tile_rows - 1) // tile_rows, cap // tile_rows)
                at = jnp.concatenate([jnp.minimum(starts, cap), tiles[None]])
                count = jnp.minimum(jnp.minimum(my_pad, slots), jnp.maximum(cap - base, 0)) // ALIGN
                return at.astype(jnp.int32), jnp.concatenate([base, count]).astype(jnp.int32)

            positions.append(pos)
            fast_meta.append([limits(*room) for room in LEVELS])
            full_meta.append(limits(ep * n, n, (SPARE_TILE,)))

            own = ids_t[:, b : b + n]
            own_hit = own[None] == experts[:, None, None]
            own_rank = rank(own_hit.any(axis=1))
            own_slot = jnp.sum(jnp.where(own_hit, own_rank[:, None], 0), axis=0)
            fast_rows.append([(own * level[1] + own_slot).T for level in LEVELS])
            full_rows.append((own * n + own_slot).T)

        def reduce(y):
            return lax.psum_scatter(y, "tp", scatter_dimension=1, tiled=True)

        def swap(y):
            return lax.all_to_all(y, "ep", 0, 0, tiled=True)

        def spare(hall0):
            n = PIECES[0]
            stacked = jax.tree.map(lambda *a: jnp.stack(a), *zip(full_meta, positions, full_rows))

            def body(p, out):
                (meta, spread_meta), pos, own_row = jax.tree.map(lambda a: lax.dynamic_index_in_dim(a, p, 0, False), stacked)
                h = norm_rows(0, n, p.reshape(1), tokens, gain2)
                hall = lax.all_gather(h, "ep", axis=0, tiled=True)
                y = reduce(ffn_piece(1, ep * n, SPARE_TILE, (n, 0), n // CHUNK, meta, pos, hall, w13, w2))
                y = swap(spread_piece(n, ep, spread_meta, y).reshape(ep, n, cols))
                o = mix_piece(n, jnp.stack([col, p]), y, tokens, own_row, gates)
                o = lax.all_gather(o, "tp", axis=1, tiled=True)
                return lax.dynamic_update_slice_in_dim(out, o, p * n, 0)

            return lax.fori_loop(0, len(PIECES), body, unwritten(tokens))

        def fast(level, hall0):
            cap, slots, *tilings = LEVELS[level]
            last, halls, reds, backs = None, {0: hall0}, {}, {}
            for step in ORDER:
                kind, names = step[0], [int(c) for c in step[1:]]
                p = names[0]
                if kind == "A":
                    halls[p] = gather_group(p, normed[p] if last is None else after(normed[p], last))
                elif kind == "F":
                    g, at = home[p]
                    hall = halls[g] if last is None else after(halls[g], last)
                    rows_of, per_block = (sum(GROUPS[g][0]), at), PIECES[p] // CHUNK
                    tile_rows, unroll = tilings[min(p, 1)]
                    last = ffn_piece(unroll, cap, tile_rows, rows_of, per_block, fast_meta[p][level][0], positions[p], hall, w13, w2)
                    reds[p] = reduce(last)
                elif kind == "S":
                    last = spread_piece(slots, ep, fast_meta[p][level][1], after(reds[p], last))
                    backs[p] = last.reshape(ep, slots, cols)
                    if p < len(PIECES) - 1:
                        backs[p] = swap(backs[p])
                else:
                    rows = [after(backs[q], last).reshape(-1, cols) for q in names[:-1]]
                    own_rows = jnp.concatenate([fast_rows[q][level] for q in names])
                    out = mix_share(tp, rows, backs[names[-1]], tokens, own_rows, gates, level)
            return out

        need = jnp.int32(0)
        for i, (cap, slots, *_) in enumerate(LEVELS):
            over = (functools.reduce(jnp.maximum, most_rows) > cap) | (functools.reduce(jnp.maximum, most_slots) > slots)
            need = jnp.where(over, i + 1, need)
        if mesh.shape["dp"] > 1:
            need = lax.pmax(need, "dp")
        paths = [functools.partial(fast, i) for i in range(len(LEVELS))]
        return lax.switch(need, [*paths, spare], hall0)

    return jax.shard_map(
        local_block,
        mesh=mesh,
        in_specs=(tok_spec, tok_spec, P(None), P(None, None), P("ep", None, "tp"), P("ep", None, "tp"), P("ep", "tp", None)),
        out_specs=tok_spec,
        check_vma=False,
    )
```

time: 2220 us -> 565 us (0.25)
  waiting for transfers between devices: 891 us -> 104 us
  local copies, waits for them, and re-layouts: 443 us -> 13.9 us
  Pallas kernels: 0 us -> 328 us
  blocking collectives: 377 us -> 59.7 us
  other arithmetic: 282 us -> 17.3 us
  matrix products: 190 us -> 1.45 us
    psum x1 -> x0, waiting for transfers between devices: 561 us -> none  [local_block(): full_out = lax.psum(part_out, 'tp')]
    pallas_call x0 -> x16, Pallas kernels: none -> 328 us  [the longest x4 167 us: ffn_piece(): pl.pallas_call(functools.partial(ffn_kernel, unroll, tile_rows, rows_of,...]
    all_to_all x1, blocking collectives: 377 us -> 59.7 us  [swap(): return lax.all_to_all(y, 'ep', 0, 0, tiled=True)]
    all_to_all x1 -> x2, waiting for transfers between devices: 330 us -> 52.2 us  [swap(): return lax.all_to_all(y, 'ep', 0, 0, tiled=True)]
    unnamed x3 -> x0, other arithmetic: 196 us -> none
    dot_general x4 -> x8, matrix products: 190 us -> 1.45 us  [rank(): jnp.dot(mask.astype(jnp.bfloat16), before, preferred_element_type=jnp.flo...]
    gather x7 -> x0, local copies, waits for them, and re-layouts: 188 us -> none  [the longest x1 95.6 us: local_block(): back_buf[dest_pos].reshape(num_tok, top_k, model_dim).astype(jnp.float32)]
    unnamed x21 -> x17, local copies, waits for them, and re-layouts: 145 us -> 10.3 us
  transfers between devices with their start and end apart: 2 -> 9, of which waited for: 2 -> 4; matrix products, arithmetic and copies ran while one was open for 1% -> 4% of each run, Pallas kernels for 0% -> 45%
where the time goes in v1:
time: 565 us; the launch traced here: 561 us
  Pallas kernels  328 us (58%)
  waiting for transfers between devices  104 us (18%)
  blocking collectives  59.7 us (11%)
  between operations  25.1 us (4%)
  other arithmetic  17.3 us (3%)
  local copies, waits for them, and re-layouts  13.9 us (2%)
  starting transfers between devices  10.7 us (2%)
    pallas_call x4, Pallas kernels, ffn_piece(): pl.pallas_call(functools.partial(ffn_kernel, unroll, tile_rows, rows_of,...  167 us
    pallas_call x1, Pallas kernels, mix_share(): pl.pallas_call(functools.partial(mix_share_kernel, peers, homes, count),...  75.3 us
    all_to_all x1, blocking collectives, swap(): return lax.all_to_all(y, 'ep', 0, 0, tiled=True)  59.7 us
    all_to_all x2, waiting for transfers between devices, swap(): return lax.all_to_all(y, 'ep', 0, 0, tiled=True)  52.2 us
    all_gather x3, waiting for transfers between devices, gather_group(): lax.all_gather(h, ('ep', 'tp') if GROUPS[g][1] else 'ep', axis=0, tiled=T...  50.2 us
    pallas_call x1, Pallas kernels, gate_rows(): pl.pallas_call(gate_kernel, grid=(rows // blk,), in_specs=[pl.BlockSpec((...  24.4 us
    pallas_call x4, Pallas kernels, spread_piece(): pl.pallas_call(functools.partial(spread_kernel, cap_slots), grid_spec=plt...  16.9 us
    pallas_call x3, Pallas kernels, norm_rows(): pl.pallas_call(norm_kernel, grid_spec=pltpu.PrefetchScalarGridSpec(num_sc...  14.6 us
  transfers between devices with their start and end apart: 9, of which 4 were waited for; matrix products, arithmetic and copies ran while one was open for 4% of the time, Pallas kernels for 45%

profile of v1, /device:TPU:97, one launch (start us, length us, event | category | flops | bytes accessed | tf_op | source)
XLA Modules:
  0.0 561.2 jit_solution(9427209405729658079)
XLA Ops:
  7.4 0.7 reshape.175.gain_ref
  8.1 2.3 norm.8
  10.5 8.5 %tell.1 = s32[8,2,2048]{2,1,0:T(2,128)} custom-call(s32[2,2048]{1,0:T(2,128)} %bitcast.118), custom_call_target="tpu_custom_call" | custom-call | flops 1048576 | bytes 262144 | tf_op jit(solution)/shard_map/tell/pallas_call | solution.py:479
  19.0 1.0 compare_reduce_fusion
  20.2 0.7 fusion.50
  21.9 0.7 fusion.46
  24.7 1.4 copy.76.ids_ref
  30.5 0.8 fusion.54
  31.9 0.7 fusion.40
  32.7 0.7 reduce_max.72
  33.4 0.7 reduce_max.73
  34.6 0.7 fusion.38
  35.3 0.7 reduce_max.74
  41.7 0.9 pad.4.rw_ref
  42.6 7.6 %block.1 = bf16[8,1408,256]{2,1,0:T(8,128)(2,1)} custom-call(bf16[1408,2048]{1,0:T(8,128)(2,1)} %bitcast.113), custom_call_target="tpu_custom_call" | custom-call | flops 11534336 | bytes 11534336 | tf_op jit(solution)/shard_map/block/pallas_call | solution.py:225
  50.2 13.9 %pair.1 = bf16[11,2048,256]{2,1,0:T(8,128)(2,1)} custom-call(bf16[2048,1408]{1,0:T(8,128)(2,1)} %bitcast.114, bf16[2048,1408]{1,0:T(8,128)(2,1)} %bitcast.115), custom_call_target="tpu_custom_call" | custom-call | flops 23068672 | bytes 23068672 | tf_op jit(solution)/shard_map/pair/pallas_call | solution.py:207
  64.2 24.4 %gate.1 = f32[2048,128]{1,0:T(8,128)} custom-call(bf16[2048,2048]{1,0:T(8,128)(2,1)} %x_ref.7, s32[2048,2]{1,0:T(8,128)} %copy.76.ids_ref, bf16[1,2048]{1,0:T(2,128)(2,1)S(1)} %reshape.175.gain_ref, bf16[2048,128]{1,0:T(8,128)(2,1)} %pad.4.rw_ref), custom_call_target="tpu_custom_call" | custom-call | flops 1073741824 | bytes 8388608 | tf_op jit(solution)/shard_map/gate/pallas_call | solution.py:68
  88.6 0.7 pad_add_fusion.24
  89.3 0.7 pad_add_fusion.25
  90.0 0.7 pad_add_fusion.26
  91.3 0.7 pad_add_fusion.30
  91.9 0.7 pad_add_fusion.29
  92.6 0.7 pad_add_fusion.28
  94.8 0.6 add_bitcast_fusion
  95.4 6.2 %norm.9 = bf16[512,2048]{1,0:T(8,128)(2,1)} custom-call(s32[1]{0:T(128)} %constant.367.clone.1.at_ref, bf16[2048,2048]{1,0:T(8,128)(2,1)} %x_ref.7, bf16[1,2048]{1,0:T(2,128)(2,1)S(1)} %reshape.175.gain_ref), custom_call_target="tpu_custom_call" | custom-call | flops 8388608 | bytes 4194304 | tf_op jit(solution)/shard_map/norm/pallas_call | solution.py:36
  101.6 6.1 %norm.10 = bf16[512,2048]{1,0:T(8,128)(2,1)} custom-call(s32[1]{0:T(128)} %constant.367.clone.1.at_ref, bf16[2048,2048]{1,0:T(8,128)(2,1)} %x_ref.7, bf16[1,2048]{1,0:T(2,128)(2,1)S(1)} %reshape.175.gain_ref), custom_call_target="tpu_custom_call" | custom-call | flops 8388608 | bytes 4194304 | tf_op jit(solution)/shard_map/norm/pallas_call | solution.py:36
  108.4 0.6 pad_add_fusion.17
  109.6 0.6 pad_add_fusion.15
  110.5 13.0 %all-gather.16.cloned.1.call-done = bf16[8192,2048]{1,0:T(8,128)(2,1)} async-done(((bf16[256,2048]{1,0:T(8,128)(2,1)}), bf16[8192,2048]{1,0:T(8,128)(2,1)}) %all-gather.16.cloned.1.call-update) | async-done | bytes 33554448 | tf_op jit(solution)/shard_map/all_gather | solution.py:529
  123.5 421.8 %conditional.1 = (bf16[2048,2048]{1,0:T(8,128)(2,1)}) conditional(s32[]{:T(128)} %clamp.3, (s32[17]{0:T(128)S(1)}, s32[16,1,256]{2,0,1:T(8,128)S(1)}, bf16[8192,2048]{1,0:T(8,128)(2,1)}, bf16[11,2048,256]{2,1,0:T(8,128)(2,1)}, bf16[8,1408,256]{2,1,0:T(8,128)(2,1)}, /*index=5*/bf16[512,2048]{1,0:T(8,128)(2,1)}, ...), branch_computations={%region_44.49_spmd, %region_49.54_spmd, %region_54.58_spmd} | conditional | flops 103754514432 | bytes 427100576 | solution.py:636
  123.5 0.8 all-gather.8.cloned.1.call-update
  124.4 40.1 %ffn.13 = bf16[1536,2048]{1,0:T(8,128)(2,1)} custom-call(s32[17]{0:T(128)S(1)} %get-tuple-element.321.meta_ref, s32[16,1,256]{2,1,0:T(1,128)S(1)} %copy.77.pos_ref, bf16[8192,2048]{1,0:T(8,128)(2,1)} %get-tuple-element.331.hall_ref, bf16[11,2048,256]{2,1,0:T(8,128)(2,1)} %get-tuple-element.324.w13_hbm, bf16[8,1408,256]{2,1,0:T(8,128)(2,1)} %get-tuple-element.325.w2_hbm), custom_call_target="tpu_custom_call" | custom-call | flops 19931332608 | bytes 39845888 | tf_op jit(solution)/shard_map/cond/branch_0_fun/ffn/pallas_call | solution.py:175
  164.6 0.7 all-gather.10.cloned.1.call-update
  165.4 42.4 %ffn.14 = bf16[1536,2048]{1,0:T(8,128)(2,1)} custom-call(s32[17]{0:T(128)S(1)} %get-tuple-element.329.meta_ref, s32[16,1,256]{2,1,0:T(1,128)S(1)} %copy.78.pos_ref, bf16[8192,2048]{1,0:T(8,128)(2,1)} %get-tuple-element.331.hall_ref, bf16[11,2048,256]{2,1,0:T(8,128)(2,1)} %get-tuple-element.324.w13_hbm, bf16[8,1408,256]{2,1,0:T(8,128)(2,1)} %get-tuple-element.325.w2_hbm), custom_call_target="tpu_custom_call" | custom-call | flops 19931332608 | bytes 39845888 | tf_op jit(solution)/shard_map/cond/branch_0_fun/ffn/pallas_call | solution.py:175
  208.0 42.7 %ffn.15 = bf16[1536,2048]{1,0:T(8,128)(2,1)} custom-call(s32[17]{0:T(128)S(1)} %get-tuple-element.326.meta_ref, s32[16,1,256]{2,1,0:T(1,128)S(1)} %copy.79.pos_ref, bf16[4096,2048]{1,0:T(8,128)(2,1)} %all-gather.8.cloned.1.call-done.hall_ref, bf16[11,2048,256]{2,1,0:T(8,128)(2,1)} %get-tuple-element.324.w13_hbm, bf16[8,1408,256]{2,1,0:T(8,128)(2,1)} %get-tuple-element.325.w2_hbm), custom_call_target="tpu_custom_call" | custom-call | flops 19931332608 | bytes 23068672 | tf_op jit(solution)/shard_map/cond/branch_0_fun/ffn/pallas_call | solution.py:175
  250.9 4.2 spread.13
  255.1 37.2 %all-gather.10.cloned.1.call-done.hall_ref = bf16[4096,2048]{1,0:T(8,128)(2,1)} async-done(((bf16[512,2048]{1,0:T(8,128)(2,1)}), bf16[4096,2048]{1,0:T(8,128)(2,1)}) %all-gather.10.cloned.1.call-update) | async-done | bytes 16777232 | tf_op jit(solution)/shard_map/cond/branch_0_fun/all_gather | solution.py:529
  292.3 42.0 %ffn.16 = bf16[1536,2048]{1,0:T(8,128)(2,1)} custom-call(s32[17]{0:T(128)S(1)} %get-tuple-element.335.meta_ref, s32[16,1,256]{2,1,0:T(1,128)S(1)} %copy.80.pos_ref, bf16[4096,2048]{1,0:T(8,128)(2,1)} %all-gather.10.cloned.1.call-done.hall_ref, bf16[11,2048,256]{2,1,0:T(8,128)(2,1)} %get-tuple-element.324.w13_hbm, bf16[8,1408,256]{2,1,0:T(8,128)(2,1)} %get-tuple-element.325.w2_hbm), custom_call_target="tpu_custom_call" | custom-call | flops 19931332608 | bytes 23068672 | tf_op jit(solution)/shard_map/cond/branch_0_fun/ffn/pallas_call | solution.py:175
  334.3 4.1 spread.14
  338.5 59.7 %all_to_all.30 = bf16[8,304,512]{2,1,0:T(8,128)(2,1)S(1)} all-to-all(bf16[8,304,512]{2,1,0:T(8,128)(2,1)} %bitcast.112), channel_id=1, replica_groups=mesh['dp'=1,'tp'=4,'ep'=8] {'ep'}, dimensions={0} | all-to-all | bytes 4980736 | tf_op jit(solution)/shard_map/cond/branch_0_fun/all_to_all | solution.py:585
  398.1 5.1 all-to-all-start
  403.3 4.4 spread.15
  407.6 26.3 %all-to-all-done = bf16[8,304,512]{2,1,0:T(8,128)(2,1)} async-done(((bf16[8,304,512]{2,1,0:T(8,128)(2,1)}), bf16[8,304,512]{2,1,0:T(8,128)(2,1)}, u32[]{:S(2)}, u32[]{:S(2)}) %all-to-all-start) | async-done | bytes 2490400 | tf_op jit(solution)/shard_map/cond/branch_0_fun/all_to_all | solution.py:585
  433.9 5.2 all-to-all-start.2
  439.6 4.2 spread.16
  443.8 26.0 %all-to-all-done.2 = bf16[8,304,512]{2,1,0:T(8,128)(2,1)} async-done(((bf16[8,304,512]{2,1,0:T(8,128)(2,1)}), bf16[8,304,512]{2,1,0:T(8,128)(2,1)}, u32[]{:S(2)}, u32[]{:S(2)}) %all-to-all-start.2) | async-done | bytes 2490400 | tf_op jit(solution)/shard_map/cond/branch_0_fun/all_to_all | solution.py:585
  469.8 75.3 %branch_0_fun.1 = bf16[2048,2048]{1,0:T(8,128)(2,1)} custom-call(bf16[2432,512]{1,0:T(8,128)(2,1)} %bitcast.1.refs_0_, bf16[2432,512]{1,0:T(8,128)(2,1)S(1)} %bitcast.105, bf16[2432,512]{1,0:T(8,128)(2,1)} %bitcast.5.refs_2_, bf16[8,304,512]{2,1,0:T(8,128)(2,1)} %bitcast.117, s32[2048,2]{1,0:T(8,128)S(1)} %copy.68.refs_4_, ...), custom_call_target="tpu_custom_call" | custom-call | flops 10200547328 | bytes 16777216 | tf_op jit(solution)/shard_map/cond/branch_0_fun/pallas_call | solution.py:433
  545.3 8.5 %copy.99 = bf16[2048,2048]{1,0:T(8,128)(2,1)} copy(bf16[2048,2048]{1,0:T(8,128)(2,1)} %get-tuple-element.422) | data formatting | bytes 16777216
  (106 shorter events, 9.1 us)
Async XLA Ops:
  7.4 17.3 %copy-start.4 = (s32[2048,2]{0,1:T(2,128)S(1)}, s32[2048,2]{0,1:T(2,128)}, u32[]{:S(2)}) copy-start(s32[2048,2]{0,1:T(2,128)} %param.13) | copy-start | bytes 49156
  7.4 116.1 %all-gather.16.cloned.1.call-start = ((), (), s32[]{:S(2)}) async-start(), calls=%async_computation.28 | async-start | bytes 34603008 | tf_op jit(solution)/shard_map/all_gather | solution.py:529
  8.1 93.5 %copy-start.2 = (bf16[1,2048]{1,0:T(2,128)(2,1)}, bf16[1,2048]{1,0:T(2,128)(2,1)S(1)}, u32[]{:S(2)}) copy-start(bf16[1,2048]{1,0:T(2,128)(2,1)S(1)} %reshape.175.gain_ref) | copy-start | bytes 12292
  8.1 21.8 %copy-start.13 = (bf16[2048,8]{0,1:T(8,128)(2,1)S(1)}, bf16[2048,8]{0,1:T(8,128)(2,1)}, u32[]{:S(2)}) copy-start(bf16[2048,8]{0,1:T(8,128)(2,1)} %param.15) | copy-start | bytes 98308
  28.4 2.0 copy-start.5
  28.8 1.6 copy-start.7
  29.3 1.2 copy-start.9
  29.8 0.6 copy-start.11
  123.5 84.5 %all-gather.8.cloned.1.call-start = ((), (), s32[]{:S(2)}) async-start(), calls=%async_computation.17 | async-start | bytes 18874368 | tf_op jit(solution)/shard_map/cond/branch_0_fun/all_gather | solution.py:529
  124.3 126.6 %reduce-scatter.10.cloned.1.call-start = ((), (), s32[]{:S(2)}) async-start(), calls=%async_computation.16 | async-start | bytes 7864320 | tf_op jit(solution)/shard_map/cond/branch_0_fun/reduce_scatter | solution.py:582
  164.5 127.7 %all-gather.10.cloned.1.call-start = ((), (), s32[]{:S(2)}) async-start(), calls=%async_computation.18 | async-start | bytes 18874368 | tf_op jit(solution)/shard_map/cond/branch_0_fun/all_gather | solution.py:529
  165.3 169.0 %reduce-scatter.16.cloned.1.call-start = ((), (), s32[]{:S(2)}) async-start(), calls=%async_computation.21 | async-start | bytes 7864320 | tf_op jit(solution)/shard_map/cond/branch_0_fun/reduce_scatter | solution.py:582
  207.9 195.4 %reduce-scatter.14.cloned.1.call-start = ((), (), s32[]{:S(2)}) async-start(), calls=%async_computation.20 | async-start | bytes 7864320 | tf_op jit(solution)/shard_map/cond/branch_0_fun/reduce_scatter | solution.py:582
  250.8 188.8 %reduce-scatter.12.cloned.1.call-start = ((), (), s32[]{:S(2)}) async-start(), calls=%async_computation.19 | async-start | bytes 7864320 | tf_op jit(solution)/shard_map/cond/branch_0_fun/reduce_scatter | solution.py:582
  398.1 35.8 %all-to-all-start = ((bf16[8,304,512]{2,1,0:T(8,128)(2,1)}), bf16[8,304,512]{2,1,0:T(8,128)(2,1)}, u32[]{:S(2)}, u32[]{:S(2)}) async-start(bf16[8,304,512]{2,1,0:T(8,128)(2,1)} %bitcast.110), calls=%async_computation.1 | async-start | bytes 4980736 | tf_op jit(solution)/shard_map/cond/branch_0_fun/all_to_all | solution.py:585
  433.9 35.9 %all-to-all-start.2 = ((bf16[8,304,512]{2,1,0:T(8,128)(2,1)}), bf16[8,304,512]{2,1,0:T(8,128)(2,1)}, u32[]{:S(2)}, u32[]{:S(2)}) async-start(bf16[8,304,512]{2,1,0:T(8,128)(2,1)} %bitcast.111), calls=%async_computation.6 | async-start | bytes 4980736 | tf_op jit(solution)/shard_map/cond/branch_0_fun/all_to_all | solution.py:585
Sparse Core Ops, SparseCore 0:
  10.6 112.8 all-gather.15
  126.0 81.6 all-gather.7
  209.3 82.9 all-gather.9
Sparse Core Ops, SparseCore 1:
  164.6 70.2 reduce-scatter.9
  237.0 61.1 reduce-scatter.15
  300.4 61.1 reduce-scatter.13
  363.9 61.1 reduce-scatter.11
